TPU v7x, 32 devices: a whole 2x2x4 slice. The times are simulated.
32 devices in a mesh: dom: 8 (over z, y), ray: 4 (over x, core).
Axes of the slice: x: 2, y: 2, z: 4, core: 2. Of those that a mesh axis runs over, the one named last changes fastest.
Arguments:
- projections: bfloat16 [8, 64, 8192], P('dom', None, 'ray'), may hold values from -6 to 6
- phase_kernel: bfloat16 [129], replicated, may hold values from -0.5 to 0.5
- image: bfloat16 [16384, 64], P('dom'), may hold values from -6 to 6
- tile_library: bfloat16 [8, 4, 16, 128, 128], P('dom', 'ray'), may hold values from -0.09375 to 0.09375
- tile_entry: int32 [8, 4, 256], P('dom', 'ray'), may hold values from 0 to 15
- tile_image: int32 [8, 4, 256], P('dom', 'ray'), may hold values from 0 to 15
- tile_slot: int32 [8, 4, 256], P('dom', 'ray'), may hold values from 0 to 7
- tile_count: int32 [8, 4], P('dom', 'ray'), may hold values from 64 to 256, as said below
- slot_block: int32 [8, 4, 8], P('dom', 'ray'), may hold values from 0 to 15
Outputs:
- residual: bfloat16 [8, 64, 8192], P('dom', None, 'ray')
- image_next: float32 [16384, 64], P(('dom', 'ray'))
Inputs may be any that keep to these rules, and one draw needn't show every extreme that they name: `tile_count`: each device has at most 256 live tiles; some device holds exactly 256. Entries beyond a device's count are not used.
All inputs are finite; a program needn't handle non-finite values.
Results may differ from a plain program's by a relative error of at most 0.0075.
Values may be sent and summed in bfloat16 or wider, within the bound.
A program may use at most 64 MiB of HBM per device.

v0:
```python
import jax
import jax.numpy as jnp
from jax import lax
from jax.sharding import PartitionSpec as P

SMOOTH = 8


relax_factor = 0.25


def with_halo(cells, sides, width):
    for axis, dim in sides:
        count = lax.axis_size(axis)
        ends = count - 1
        head = lax.slice_in_dim(cells, 0, width, axis=dim)
        tail = lax.slice_in_dim(cells, cells.shape[dim] - width, cells.shape[dim], axis=dim)
        cells = jnp.concatenate(
            [
                lax.ppermute(tail, axis, [(i, (i + 1) % count) for i in range(ends)]),
                cells,
                lax.ppermute(head, axis, [((i + 1) % count, i) for i in range(ends)]),
            ],
            axis=dim,
        )
    return cells


def toeplitz(kernel, tile_size):
    taps = kernel.shape[0]
    padded = jnp.concatenate([kernel, jnp.zeros((2 * tile_size + 1 - taps,), kernel.dtype)])
    tiled = jnp.tile(padded, tile_size)[: 2 * tile_size * tile_size]
    return tiled.reshape(tile_size, 2 * tile_size).T


def phase_filter(projections, phase_kernel, tile_size):
    half_width = (phase_kernel.shape[0] - 1) // 2
    angles, slices, columns = projections.shape
    block_count = columns // tile_size
    rimmed = with_halo(projections, (("ray", 2),), half_width)
    padded = jnp.pad(rimmed, ((0, 0), (0, 0), (0, 2 * tile_size - 2 * half_width)))
    blocks = padded.reshape(angles, slices, block_count + 2, tile_size)
    windows = jnp.concatenate(
        [blocks[:, :, :block_count], blocks[:, :, 1 : block_count + 1]], axis=-1
    )
    filtered = jnp.einsum(
        "asbi,ij->asbj",
        windows,
        toeplitz(phase_kernel, tile_size),
        preferred_element_type=jnp.float32,
    )
    return filtered.reshape(angles, slices, columns).astype(jnp.bfloat16)


def stripe_profile(gathered):
    profile = jnp.median(gathered.astype(jnp.float32), axis=0)
    columns = profile.shape[1]
    rimmed = with_halo(profile, (("ray", 1),), SMOOTH)
    window_sum = jnp.zeros_like(profile)
    for offset in range(2 * SMOOTH + 1):
        window_sum = window_sum + rimmed[:, offset : offset + columns]
    position = lax.axis_index("ray") * columns + jnp.arange(columns)
    detector = lax.axis_size("ray") * columns
    in_range = (
        jnp.minimum(position + SMOOTH, detector - 1) - jnp.maximum(position - SMOOTH, 0) + 1
    ).astype(jnp.float32)
    return (profile - window_sum / in_range).astype(jnp.bfloat16)


def shards(
    projections,
    phase_kernel,
    image,
    tile_library,
    tile_entry,
    tile_image,
    tile_slot,
    tile_count,
    slot_block,
):
    tile_size = tile_library.shape[-1]
    angles, slices, columns = projections.shape
    phase = phase_filter(projections, phase_kernel, tile_size)
    gathered = lax.all_to_all(phase, "dom", split_axis=1, concat_axis=0, tiled=True)
    stripe = stripe_profile(gathered)
    fixed_rows = (gathered.astype(jnp.float32) - stripe.astype(jnp.float32)[None]).astype(
        jnp.bfloat16
    )
    corrected = lax.all_to_all(fixed_rows, "dom", split_axis=0, concat_axis=1, tiled=True)
    owners = lax.axis_size("dom")
    library = tile_library[0, 0]
    entries = tile_entry[0, 0]
    images = tile_image[0, 0]
    slots = tile_slot[0, 0]
    capacity = entries.shape[0]
    block_size = 64
    turn_count = capacity // block_size
    image_blocks = image.reshape(-1, tile_size, slices)
    block_total = image_blocks.shape[0]
    live_mask = jnp.arange(capacity) < tile_count[0, 0]
    slot_target = jnp.where(live_mask, slots, owners)
    image_target = jnp.where(live_mask, images, block_total)

    def forward_turn(turn_index, partial_value):
        first_tile = turn_index * block_size
        chosen = lax.dynamic_slice_in_dim(entries, first_tile, block_size)
        placed = lax.dynamic_slice_in_dim(images, first_tile, block_size)
        destined = lax.dynamic_slice_in_dim(slot_target, first_tile, block_size)
        product = jnp.einsum(
            "krp,kps->ksr",
            library[chosen],
            image_blocks[placed],
            preferred_element_type=jnp.float32,
        )
        return partial_value.at[destined].add(product, mode="drop")

    partial_value = lax.fori_loop(
        0, turn_count, forward_turn, jnp.zeros((owners, slices, tile_size), jnp.float32)
    )
    received = lax.all_to_all(
        partial_value.astype(jnp.bfloat16), "dom", split_axis=0, concat_axis=0, tiled=True
    )
    per_owner = columns // tile_size
    carried = slot_block[0, 0]
    block_ids = jnp.arange(angles * per_owner).reshape(angles, per_owner)
    selector = (block_ids[:, :, None] == carried[None, None, :]).astype(jnp.bfloat16)
    forward = jnp.einsum("abd,dst->asbt", selector, received, preferred_element_type=jnp.float32)
    residual = (corrected.astype(jnp.float32) - forward.reshape(angles, slices, columns)).astype(
        jnp.bfloat16
    )
    back = jnp.einsum(
        "abd,asbt->dst",
        selector,
        residual.reshape(angles, slices, per_owner, tile_size),
        preferred_element_type=jnp.float32,
    ).astype(jnp.bfloat16)
    returned = lax.all_to_all(back, "dom", split_axis=0, concat_axis=0, tiled=True)

    def adjoint_turn(turn_index, gradient):
        first_tile = turn_index * block_size
        chosen = lax.dynamic_slice_in_dim(entries, first_tile, block_size)
        sourced = lax.dynamic_slice_in_dim(slots, first_tile, block_size)
        destined = lax.dynamic_slice_in_dim(image_target, first_tile, block_size)
        product = jnp.einsum(
            "krp,ksr->kps", library[chosen], returned[sourced], preferred_element_type=jnp.float32
        )
        return gradient.at[destined].add(product, mode="drop")

    gradient = lax.fori_loop(
        0, turn_count, adjoint_turn, jnp.zeros((block_total, tile_size, slices), jnp.float32)
    )
    gradient = gradient.reshape(-1, slices)
    rows_own = gradient.shape[0] // lax.axis_size("ray")
    update = lax.psum_scatter(gradient, "ray", scatter_dimension=0, tiled=True)
    own_image = lax.dynamic_slice_in_dim(image, lax.axis_index("ray") * rows_own, rows_own)
    image_next = own_image.astype(jnp.float32) + relax_factor * update
    return (residual, image_next)


def solution(mesh):
    return jax.shard_map(
        shards,
        mesh=mesh,
        in_specs=(
            P("dom", None, "ray"),
            P(),
            P("dom", None),
            P("dom", "ray", None, None, None),
            P("dom", "ray", None),
            P("dom", "ray", None),
            P("dom", "ray", None),
            P("dom", "ray"),
            P("dom", "ray", None),
        ),
        out_specs=(P("dom", None, "ray"), P(("dom", "ray"), None)),
        check_vma=False,
    )
```

profile of v0, /device:TPU:0, one launch (start us, length us, event | category | flops | bytes accessed | tf_op | source)
XLA Modules:
  0.0 195.9 jit_solution(8649035580683881368)
XLA Ops:
  7.2 0.8 fusion.53
  8.0 2.4 %collective-permute-start = (bf16[1,64,64]{2,1,0:T(8,128)(2,1)S(1)}, bf16[1,64,64]{2,1,0:T(8,128)(2,1)S(1)}, u32[]{:S(2)}, u32[]{:S(2)}) collective-permute-start(bf16[1,64,64]{2,1,0:T(8,128)(2,1)S(1)} %get-tuple-element.333), channel_id=1, source_target_pairs={{0,1},{1,2},{2,3},{4,5},{5,6},{6,7},{8,9},{9,10},{10,11},{12,13},{... | collective-permute-start | bytes 24584 | tf_op jit(solution)/shard_map/ppermute | solution.py:20
  10.4 1.3 collective-permute-start.1
  12.3 0.7 fusion.50
  13.0 1.2 copy.32
  14.2 0.7 concatenate.32
  15.5 1.2 concatenate.30
  17.6 0.5 broadcast.188
  18.1 2.2 %reduce = bf16[64,2048]{1,0:T(8,128)(2,1)S(1)} reduce(bf16[64,1,2048]{2,1,0:T(2,128)(2,1)S(1)} %bitcast.81, bf16[]{:T(256)} %broadcast.188), dimensions={1}, to_apply=%bitcast.54.reduce_sub_computation | reduce | bytes 524290
  20.2 1.0 reshape.296
  21.2 6.4 %all-to-all-start = ((bf16[8,2,8192]{2,1,0:T(2,128)(2,1)}), bf16[8,2,8192]{2,1,0:T(2,128)(2,1)}, u32[]{:S(2)}, u32[]{:S(2)}) async-start(bf16[8,2,8192]{2,1,0:T(2,128)(2,1)} %reshape.296), calls=%async_computation | async-start | bytes 524288 | tf_op jit(solution)/shard_map/all_to_all | solution.py:84
  27.7 47.9 %while.28 = (s32[]{:T(128)}, f32[8,64,128]{2,1,0:T(8,128)S(1)}, s32[256]{0:T(256)S(1)}, s32[256]{0:T(256)S(1)}, bf16[16,128,64]{2,1,0:T(8,128)(2,1)S(1)}, /*inde...) while((s32[]{:T(128)}, f32[8,64,128]{2,1,0:T(8,128)S(1)}, ...), condition=%wide.region_4.5_spmd, body=%wide.region_2.4_spmd.sunk | while | flops 134744640 | bytes 17836972 | solution.py:117
  27.9 2.2 %gather_fusion = bf16[64,128,64]{2,1,0:T(8,128)(2,1)} fusion(bf16[16,128,64]{2,1,0:T(8,128)(2,1)S(1)} %get-tuple-element.456, s32[1024]{0:T(1024)S(1)} %pad_clamp_fusion.8), kind=kCustom, calls=%fused_computation.clone.1 | custom fusion | bytes 2097408 | tf_op jit(solution)/shard_map/while/body/eval_jaxpr/gather | solution.py:112
  30.1 2.1 %gather_fusion.1 = bf16[64,128,128]{2,1,0:T(8,128)(2,1)} fusion(bf16[16,128,128]{2,1,0:T(8,128)(2,1)S(1)} %get-tuple-element.458, s32[1024]{0:T(1024)S(1)} %pad_clamp_fusion.9), kind=kCustom, calls=%fused_computation.1.clone.1 | custom fusion | bytes 4194560 | tf_op jit(solution)/shard_map/while/body/eval_jaxpr/gather | solution.py:111
  32.2 3.7 %fusion.71 = f32[64,64,128]{2,1,0:T(8,128)S(1)} fusion(bf16[64,128,64]{2,1,0:T(8,128)(2,1)} %gather_fusion, bf16[64,128,128]{2,1,0:T(8,128)(2,1)} %gather_fusion.1), kind=kOutput, calls=%fused_computation.113.clone.1 | convolution fusion | flops 134217728 | bytes 5242880 | tf_op jit(solution)/shard_map/while/body/eval_jaxpr/krp,kps->ksr/dot_general | solution.py:109
  35.9 3.8 %scatter_fusion = f32[8,64,128]{2,1,0:T(8,128)S(1)} fusion(f32[8,64,128]{2,1,0:T(8,128)S(1)} %get-tuple-element.442, s32[64]{0:T(128)S(1)} %compare_select_fusion.10, f32[64,64,128]{2,1,0:T(8,128)S(1)} %fusion.71), kind=kCustom, calls=%fused_computation.4.clone.1 | custom fusion | flops 524288 | bytes 6291712 | tf_op jit(solution)/shard_map/while/body/eval_jaxpr/scatter-add | solution.py:115
  39.9 2.2 %gather_fusion = bf16[64,128,64]{2,1,0:T(8,128)(2,1)} fusion(bf16[16,128,64]{2,1,0:T(8,128)(2,1)S(1)} %get-tuple-element.456, s32[1024]{0:T(1024)S(1)} %pad_clamp_fusion.8), kind=kCustom, calls=%fused_computation.clone.1 | custom fusion | bytes 2097408 | tf_op jit(solution)/shard_map/while/body/eval_jaxpr/gather | solution.py:112
  42.0 2.1 %gather_fusion.1 = bf16[64,128,128]{2,1,0:T(8,128)(2,1)} fusion(bf16[16,128,128]{2,1,0:T(8,128)(2,1)S(1)} %get-tuple-element.458, s32[1024]{0:T(1024)S(1)} %pad_clamp_fusion.9), kind=kCustom, calls=%fused_computation.1.clone.1 | custom fusion | bytes 4194560 | tf_op jit(solution)/shard_map/while/body/eval_jaxpr/gather | solution.py:111
  44.1 3.7 %fusion.71 = f32[64,64,128]{2,1,0:T(8,128)S(1)} fusion(bf16[64,128,64]{2,1,0:T(8,128)(2,1)} %gather_fusion, bf16[64,128,128]{2,1,0:T(8,128)(2,1)} %gather_fusion.1), kind=kOutput, calls=%fused_computation.113.clone.1 | convolution fusion | flops 134217728 | bytes 5242880 | tf_op jit(solution)/shard_map/while/body/eval_jaxpr/krp,kps->ksr/dot_general | solution.py:109
  47.9 3.8 %scatter_fusion = f32[8,64,128]{2,1,0:T(8,128)S(1)} fusion(f32[8,64,128]{2,1,0:T(8,128)S(1)} %get-tuple-element.442, s32[64]{0:T(128)S(1)} %compare_select_fusion.10, f32[64,64,128]{2,1,0:T(8,128)S(1)} %fusion.71), kind=kCustom, calls=%fused_computation.4.clone.1 | custom fusion | flops 524288 | bytes 6291712 | tf_op jit(solution)/shard_map/while/body/eval_jaxpr/scatter-add | solution.py:115
  51.8 2.2 %gather_fusion = bf16[64,128,64]{2,1,0:T(8,128)(2,1)} fusion(bf16[16,128,64]{2,1,0:T(8,128)(2,1)S(1)} %get-tuple-element.456, s32[1024]{0:T(1024)S(1)} %pad_clamp_fusion.8), kind=kCustom, calls=%fused_computation.clone.1 | custom fusion | bytes 2097408 | tf_op jit(solution)/shard_map/while/body/eval_jaxpr/gather | solution.py:112
  54.0 2.1 %gather_fusion.1 = bf16[64,128,128]{2,1,0:T(8,128)(2,1)} fusion(bf16[16,128,128]{2,1,0:T(8,128)(2,1)S(1)} %get-tuple-element.458, s32[1024]{0:T(1024)S(1)} %pad_clamp_fusion.9), kind=kCustom, calls=%fused_computation.1.clone.1 | custom fusion | bytes 4194560 | tf_op jit(solution)/shard_map/while/body/eval_jaxpr/gather | solution.py:111
  56.1 3.7 %fusion.71 = f32[64,64,128]{2,1,0:T(8,128)S(1)} fusion(bf16[64,128,64]{2,1,0:T(8,128)(2,1)} %gather_fusion, bf16[64,128,128]{2,1,0:T(8,128)(2,1)} %gather_fusion.1), kind=kOutput, calls=%fused_computation.113.clone.1 | convolution fusion | flops 134217728 | bytes 5242880 | tf_op jit(solution)/shard_map/while/body/eval_jaxpr/krp,kps->ksr/dot_general | solution.py:109
  59.9 3.8 %scatter_fusion = f32[8,64,128]{2,1,0:T(8,128)S(1)} fusion(f32[8,64,128]{2,1,0:T(8,128)S(1)} %get-tuple-element.442, s32[64]{0:T(128)S(1)} %compare_select_fusion.10, f32[64,64,128]{2,1,0:T(8,128)S(1)} %fusion.71), kind=kCustom, calls=%fused_computation.4.clone.1 | custom fusion | flops 524288 | bytes 6291712 | tf_op jit(solution)/shard_map/while/body/eval_jaxpr/scatter-add | solution.py:115
  63.8 2.2 %gather_fusion = bf16[64,128,64]{2,1,0:T(8,128)(2,1)} fusion(bf16[16,128,64]{2,1,0:T(8,128)(2,1)S(1)} %get-tuple-element.456, s32[1024]{0:T(1024)S(1)} %pad_clamp_fusion.8), kind=kCustom, calls=%fused_computation.clone.1 | custom fusion | bytes 2097408 | tf_op jit(solution)/shard_map/while/body/eval_jaxpr/gather | solution.py:112
  66.0 2.1 %gather_fusion.1 = bf16[64,128,128]{2,1,0:T(8,128)(2,1)} fusion(bf16[16,128,128]{2,1,0:T(8,128)(2,1)S(1)} %get-tuple-element.458, s32[1024]{0:T(1024)S(1)} %pad_clamp_fusion.9), kind=kCustom, calls=%fused_computation.1.clone.1 | custom fusion | bytes 4194560 | tf_op jit(solution)/shard_map/while/body/eval_jaxpr/gather | solution.py:111
  68.1 3.7 %fusion.71 = f32[64,64,128]{2,1,0:T(8,128)S(1)} fusion(bf16[64,128,64]{2,1,0:T(8,128)(2,1)} %gather_fusion, bf16[64,128,128]{2,1,0:T(8,128)(2,1)} %gather_fusion.1), kind=kOutput, calls=%fused_computation.113.clone.1 | convolution fusion | flops 134217728 | bytes 5242880 | tf_op jit(solution)/shard_map/while/body/eval_jaxpr/krp,kps->ksr/dot_general | solution.py:109
  71.8 3.8 %scatter_fusion = f32[8,64,128]{2,1,0:T(8,128)S(1)} fusion(f32[8,64,128]{2,1,0:T(8,128)S(1)} %get-tuple-element.442, s32[64]{0:T(128)S(1)} %compare_select_fusion.10, f32[64,64,128]{2,1,0:T(8,128)S(1)} %fusion.71), kind=kCustom, calls=%fused_computation.4.clone.1 | custom fusion | flops 524288 | bytes 6291712 | tf_op jit(solution)/shard_map/while/body/eval_jaxpr/scatter-add | solution.py:115
  75.6 0.7 convert_element_type.108
  76.3 6.0 %all-to-all-start.2 = ((bf16[8,64,128]{2,1,0:T(8,128)(2,1)}), bf16[8,64,128]{2,1,0:T(8,128)(2,1)S(1)}, u32[]{:S(2)}, u32[]{:S(2)}) async-start(bf16[8,64,128]{2,1,0:T(8,128)(2,1)} %convert_element_type.108), calls=%async_computation.2 | async-start | bytes 262144 | tf_op jit(solution)/shard_map/all_to_all | solution.py:120
  82.3 1.2 reshape.297
  84.2 4.8 %sort.16 = (f32[8,8,2048]{2,0,1:T(8,128)S(1)}, s32[8,8,2048]{2,0,1:T(8,128)}) sort(f32[8,8,2048]{2,0,1:T(8,128)S(1)} %copy_select_fusion, s32[8,8,2048]{2,0,1:T(8,128)S(1)} %iota.19), dimensions={0}, to_apply=%region_1.2 | sort | flops 2228224 | bytes 2097152 | tf_op jit(solution)/shard_map/jit(median)/jit(quantile)/sort | solution.py:56
  89.2 1.3 collective-permute-start.3
  90.5 4.1 %collective-permute-start.2 = (f32[8,8]{1,0:T(8,128)S(1)}, f32[8,8]{1,0:T(8,128)S(1)}, u32[]{:S(2)}, u32[]{:S(2)}) collective-permute-start(f32[8,8]{1,0:T(8,128)S(1)} %get-tuple-element.334), channel_id=1, source_target_pairs={{0,1},{1,2},{2,3},{4,5},{5,6},{6,7},{8,9},{9,10},{10,11},{12,13},{... | collective-permute-start | bytes 776 | tf_op jit(solution)/shard_map/ppermute | solution.py:20
  94.6 0.8 collective-permute-done.2
  95.3 0.4 fusion.42
  95.7 0.9 subtract_convert_fusion
  96.6 5.7 %all-to-all-start.1 = ((bf16[8,8,2048]{2,1,0:T(8,128)(2,1)}), bf16[8,8,2048]{2,1,0:T(8,128)(2,1)S(1)}, u32[]{:S(2)}, u32[]{:S(2)}) async-start(bf16[8,8,2048]{2,1,0:T(8,128)(2,1)} %subtract_convert_fusion), calls=%async_computation.1 | async-start | bytes 524288 | tf_op jit(solution)/shard_map/all_to_all | solution.py:89
  102.7 8.1 %all-to-all-done.1 = bf16[8,8,2048]{2,1,0:T(8,128)(2,1)S(1)} async-done(((bf16[8,8,2048]{2,1,0:T(8,128)(2,1)}), bf16[8,8,2048]{2,1,0:T(8,128)(2,1)S(1)}, u32[]{:S(2)}, u32[]{:S(2)}) %all-to-all-start.1) | async-done | bytes 262176 | tf_op jit(solution)/shard_map/all_to_all | solution.py:89
  111.1 0.7 copy.34
  111.8 5.0 %all-to-all-start.3 = ((bf16[8,64,128]{2,1,0:T(8,128)(2,1)}), bf16[8,64,128]{2,1,0:T(8,128)(2,1)S(1)}, u32[]{:S(2)}, u32[]{:S(2)}) async-start(bf16[8,64,128]{2,1,0:T(8,128)(2,1)} %copy.34), calls=%async_computation.3 | async-start | bytes 262144 | tf_op jit(solution)/shard_map/all_to_all | solution.py:137
  116.9 7.4 %all-to-all-done.3 = bf16[8,64,128]{2,1,0:T(8,128)(2,1)S(1)} async-done(((bf16[8,64,128]{2,1,0:T(8,128)(2,1)}), bf16[8,64,128]{2,1,0:T(8,128)(2,1)S(1)}, u32[]{:S(2)}, u32[]{:S(2)}) %all-to-all-start.3) | async-done | bytes 131104 | tf_op jit(solution)/shard_map/all_to_all | solution.py:137
  124.3 41.5 %while.29 = (s32[]{:T(128)}, f32[16,128,64]{1,2,0:T(8,128)S(1)}, s32[256]{0:T(256)S(1)}, s32[256]{0:T(256)S(1)}, bf16[16,128,128]{2,1,0:T(8,128)(2,1)S(1)}, /*in...) while((s32[]{:T(128)}, f32[16,128,64]{1,2,0:T(8,128)S(1)}, ...), condition=%wide.region_7.8_spmd, body=%wide.region_5.7_spmd.sunk | while | flops 134744640 | bytes 17836972 | solution.py:149
  124.5 1.7 gather_fusion.2
  126.2 2.2 %gather_fusion.3 = bf16[64,128,128]{2,1,0:T(8,128)(2,1)} fusion(bf16[16,128,128]{2,1,0:T(8,128)(2,1)S(1)} %get-tuple-element.489, s32[1024]{0:T(1024)S(1)} %pad_clamp_fusion.11), kind=kCustom, calls=%fused_computation.2.clone.1 | custom fusion | bytes 4194560 | tf_op jit(solution)/shard_map/while/body/eval_jaxpr/gather | solution.py:145
  128.3 2.6 %fusion.74 = f32[64,128,64]{1,2,0:T(8,128)S(1)} fusion(bf16[64,64,128]{2,1,0:T(8,128)(2,1)} %gather_fusion.2, bf16[64,128,128]{2,1,0:T(8,128)(2,1)} %gather_fusion.3), kind=kOutput, calls=%fused_computation.114.clone.1 | convolution fusion | flops 134217728 | bytes 5242880 | tf_op jit(solution)/shard_map/while/body/eval_jaxpr/krp,ksr->kps/dot_general | solution.py:144
  130.9 3.7 %scatter_fusion.1 = f32[16,128,64]{1,2,0:T(8,128)S(1)} fusion(f32[16,128,64]{1,2,0:T(8,128)S(1)} %get-tuple-element.475, s32[64]{0:T(128)S(1)} %compare_select_fusion.12, f32[64,128,64]{1,2,0:T(8,128)S(1)} %fusion.74), kind=kCustom, calls=%fused_computation.5.clone.1 | custom fusion | flops 524288 | bytes 6291712 | tf_op jit(solution)/shard_map/while/body/eval_jaxpr/scatter-add | solution.py:147
  134.8 1.7 gather_fusion.2
  136.5 2.2 %gather_fusion.3 = bf16[64,128,128]{2,1,0:T(8,128)(2,1)} fusion(bf16[16,128,128]{2,1,0:T(8,128)(2,1)S(1)} %get-tuple-element.489, s32[1024]{0:T(1024)S(1)} %pad_clamp_fusion.11), kind=kCustom, calls=%fused_computation.2.clone.1 | custom fusion | bytes 4194560 | tf_op jit(solution)/shard_map/while/body/eval_jaxpr/gather | solution.py:145
  138.7 2.6 %fusion.74 = f32[64,128,64]{1,2,0:T(8,128)S(1)} fusion(bf16[64,64,128]{2,1,0:T(8,128)(2,1)} %gather_fusion.2, bf16[64,128,128]{2,1,0:T(8,128)(2,1)} %gather_fusion.3), kind=kOutput, calls=%fused_computation.114.clone.1 | convolution fusion | flops 134217728 | bytes 5242880 | tf_op jit(solution)/shard_map/while/body/eval_jaxpr/krp,ksr->kps/dot_general | solution.py:144
  141.3 3.8 %scatter_fusion.1 = f32[16,128,64]{1,2,0:T(8,128)S(1)} fusion(f32[16,128,64]{1,2,0:T(8,128)S(1)} %get-tuple-element.475, s32[64]{0:T(128)S(1)} %compare_select_fusion.12, f32[64,128,64]{1,2,0:T(8,128)S(1)} %fusion.74), kind=kCustom, calls=%fused_computation.5.clone.1 | custom fusion | flops 524288 | bytes 6291712 | tf_op jit(solution)/shard_map/while/body/eval_jaxpr/scatter-add | solution.py:147
  145.2 1.7 gather_fusion.2
  146.9 2.2 %gather_fusion.3 = bf16[64,128,128]{2,1,0:T(8,128)(2,1)} fusion(bf16[16,128,128]{2,1,0:T(8,128)(2,1)S(1)} %get-tuple-element.489, s32[1024]{0:T(1024)S(1)} %pad_clamp_fusion.11), kind=kCustom, calls=%fused_computation.2.clone.1 | custom fusion | bytes 4194560 | tf_op jit(solution)/shard_map/while/body/eval_jaxpr/gather | solution.py:145
  149.1 2.6 %fusion.74 = f32[64,128,64]{1,2,0:T(8,128)S(1)} fusion(bf16[64,64,128]{2,1,0:T(8,128)(2,1)} %gather_fusion.2, bf16[64,128,128]{2,1,0:T(8,128)(2,1)} %gather_fusion.3), kind=kOutput, calls=%fused_computation.114.clone.1 | convolution fusion | flops 134217728 | bytes 5242880 | tf_op jit(solution)/shard_map/while/body/eval_jaxpr/krp,ksr->kps/dot_general | solution.py:144
  151.6 3.8 %scatter_fusion.1 = f32[16,128,64]{1,2,0:T(8,128)S(1)} fusion(f32[16,128,64]{1,2,0:T(8,128)S(1)} %get-tuple-element.475, s32[64]{0:T(128)S(1)} %compare_select_fusion.12, f32[64,128,64]{1,2,0:T(8,128)S(1)} %fusion.74), kind=kCustom, calls=%fused_computation.5.clone.1 | custom fusion | flops 524288 | bytes 6291712 | tf_op jit(solution)/shard_map/while/body/eval_jaxpr/scatter-add | solution.py:147
  155.6 1.7 gather_fusion.2
  157.3 2.2 %gather_fusion.3 = bf16[64,128,128]{2,1,0:T(8,128)(2,1)} fusion(bf16[16,128,128]{2,1,0:T(8,128)(2,1)S(1)} %get-tuple-element.489, s32[1024]{0:T(1024)S(1)} %pad_clamp_fusion.11), kind=kCustom, calls=%fused_computation.2.clone.1 | custom fusion | bytes 4194560 | tf_op jit(solution)/shard_map/while/body/eval_jaxpr/gather | solution.py:145
  159.4 2.6 %fusion.74 = f32[64,128,64]{1,2,0:T(8,128)S(1)} fusion(bf16[64,64,128]{2,1,0:T(8,128)(2,1)} %gather_fusion.2, bf16[64,128,128]{2,1,0:T(8,128)(2,1)} %gather_fusion.3), kind=kOutput, calls=%fused_computation.114.clone.1 | convolution fusion | flops 134217728 | bytes 5242880 | tf_op jit(solution)/shard_map/while/body/eval_jaxpr/krp,ksr->kps/dot_general | solution.py:144
  162.0 3.8 %scatter_fusion.1 = f32[16,128,64]{1,2,0:T(8,128)S(1)} fusion(f32[16,128,64]{1,2,0:T(8,128)S(1)} %get-tuple-element.475, s32[64]{0:T(128)S(1)} %compare_select_fusion.12, f32[64,128,64]{1,2,0:T(8,128)S(1)} %fusion.74), kind=kCustom, calls=%fused_computation.5.clone.1 | custom fusion | flops 524288 | bytes 6291712 | tf_op jit(solution)/shard_map/while/body/eval_jaxpr/scatter-add | solution.py:147
  165.8 0.8 copy_bitcast_fusion
  166.7 1.1 reshape.187
  167.8 0.8 fusion.1
  168.5 19.0 %reduce-scatter.2.cloned.1.call-done = f32[512,64]{0,1:T(8,128)} async-done(((f32[2048,64]{0,1:T(8,128)}), f32[512,64]{0,1:T(8,128)}) %reduce-scatter.2.cloned.1.call-update) | async-done | bytes 131088 | tf_op jit(solution)/shard_map/reduce_scatter | solution.py:154
  187.5 1.6 multiply_add_fusion
  (75 shorter events, 4.5 us)
Async XLA Ops:
  8.0 7.3 %collective-permute-start = (bf16[1,64,64]{2,1,0:T(8,128)(2,1)S(1)}, bf16[1,64,64]{2,1,0:T(8,128)(2,1)S(1)}, u32[]{:S(2)}, u32[]{:S(2)}) collective-permute-start(bf16[1,64,64]{2,1,0:T(8,128)(2,1)S(1)} %get-tuple-element.333), channel_id=1, source_target_pairs={{0,1},{1,2},{2,3},{4,5},{5,6},{6,7},{8,9},{9,10},{10,11},{12,13},{... | collective-permute-start | bytes 24584 | tf_op jit(solution)/shard_map/ppermute | solution.py:20
  10.4 5.2 %collective-permute-start.1 = (bf16[1,64,64]{2,1,0:T(8,128)(2,1)S(1)}, bf16[1,64,64]{2,1,0:T(8,128)(2,1)S(1)}, u32[]{:S(2)}, u32[]{:S(2)}) collective-permute-start(bf16[1,64,64]{2,1,0:T(8,128)(2,1)S(1)} %get-tuple-element.332), channel_id=1, source_target_pairs={{1,0},{2,1},{3,2},{5,4},{6,5},{7,6},{9,8},{10,9},{11,10},{13,12},{... | collective-permute-start | bytes 24584 | tf_op jit(solution)/shard_map/ppermute | solution.py:22
  17.1 10.6 %copy-start = (bf16[1,1,16,128,128]{4,3,2,1,0:T(8,128)(2,1)S(1)}, bf16[1,1,16,128,128]{4,3,2,1,0:T(8,128)(2,1)}, u32[]{:S(2)}) copy-start(bf16[1,1,16,128,128]{4,3,2,1,0:T(8,128)(2,1)} %param.16) | copy-start | bytes 1572868
  17.1 10.6 %copy-start.2 = (s32[1,1,256]{2,1,0:T(1,128)S(1)}, s32[1,1,256]{2,1,0:T(1,128)}, u32[]{:S(2)}) copy-start(s32[1,1,256]{2,1,0:T(1,128)} %param.17) | copy-start | bytes 3076
  17.1 10.6 %copy-start.3 = (s32[1,1,256]{2,1,0:T(1,128)S(1)}, s32[1,1,256]{2,1,0:T(1,128)}, u32[]{:S(2)}) copy-start(s32[1,1,256]{2,1,0:T(1,128)} %param.18) | copy-start | bytes 3076
  21.2 55.1 %all-to-all-start = ((bf16[8,2,8192]{2,1,0:T(2,128)(2,1)}), bf16[8,2,8192]{2,1,0:T(2,128)(2,1)}, u32[]{:S(2)}, u32[]{:S(2)}) async-start(bf16[8,2,8192]{2,1,0:T(2,128)(2,1)} %reshape.296), calls=%async_computation | async-start | bytes 524288 | tf_op jit(solution)/shard_map/all_to_all | solution.py:84
  76.3 20.3 %all-to-all-start.2 = ((bf16[8,64,128]{2,1,0:T(8,128)(2,1)}), bf16[8,64,128]{2,1,0:T(8,128)(2,1)S(1)}, u32[]{:S(2)}, u32[]{:S(2)}) async-start(bf16[8,64,128]{2,1,0:T(8,128)(2,1)} %convert_element_type.108), calls=%async_computation.2 | async-start | bytes 262144 | tf_op jit(solution)/shard_map/all_to_all | solution.py:120
  83.8 18.5 %copy-start.5 = (s32[1,1,8]{2,1,0:T(1,128)S(1)}, s32[1,1,8]{2,1,0:T(1,128)}, u32[]{:S(2)}) copy-start(s32[1,1,8]{2,1,0:T(1,128)} %param.21) | copy-start | bytes 100
  89.2 5.4 %collective-permute-start.3 = (f32[8,8]{1,0:T(8,128)S(1)}, f32[8,8]{1,0:T(8,128)S(1)}, u32[]{:S(2)}, u32[]{:S(2)}) collective-permute-start(f32[8,8]{1,0:T(8,128)S(1)} %get-tuple-element.335), channel_id=1, source_target_pairs={{1,0},{2,1},{3,2},{5,4},{6,5},{7,6},{9,8},{10,9},{11,10},{13,12},{... | collective-permute-start | bytes 776 | tf_op jit(solution)/shard_map/ppermute | solution.py:22
  90.5 4.9 %collective-permute-start.2 = (f32[8,8]{1,0:T(8,128)S(1)}, f32[8,8]{1,0:T(8,128)S(1)}, u32[]{:S(2)}, u32[]{:S(2)}) collective-permute-start(f32[8,8]{1,0:T(8,128)S(1)} %get-tuple-element.334), channel_id=1, source_target_pairs={{0,1},{1,2},{2,3},{4,5},{5,6},{6,7},{8,9},{9,10},{10,11},{12,13},{... | collective-permute-start | bytes 776 | tf_op jit(solution)/shard_map/ppermute | solution.py:20
  96.6 14.2 %all-to-all-start.1 = ((bf16[8,8,2048]{2,1,0:T(8,128)(2,1)}), bf16[8,8,2048]{2,1,0:T(8,128)(2,1)S(1)}, u32[]{:S(2)}, u32[]{:S(2)}) async-start(bf16[8,8,2048]{2,1,0:T(8,128)(2,1)} %subtract_convert_fusion), calls=%async_computation.1 | async-start | bytes 524288 | tf_op jit(solution)/shard_map/all_to_all | solution.py:89
  102.6 9.2 %copy-start.1 = (f32[1,64,16,128]{3,2,1,0:T(8,128)}, f32[1,64,16,128]{3,2,1,0:T(8,128)S(1)}, u32[]{:S(2)}) copy-start(f32[1,64,16,128]{3,2,1,0:T(8,128)S(1)} %convolution_bitcast_fusion) | copy-start | bytes 1572868
  102.6 21.7 %copy-start.4 = (s32[1,1,256]{2,1,0:T(1,128)S(1)}, s32[1,1,256]{2,1,0:T(1,128)}, u32[]{:S(2)}) copy-start(s32[1,1,256]{2,1,0:T(1,128)} %param.19) | copy-start | bytes 3076
  111.8 12.4 %all-to-all-start.3 = ((bf16[8,64,128]{2,1,0:T(8,128)(2,1)}), bf16[8,64,128]{2,1,0:T(8,128)(2,1)S(1)}, u32[]{:S(2)}, u32[]{:S(2)}) async-start(bf16[8,64,128]{2,1,0:T(8,128)(2,1)} %copy.34), calls=%async_computation.3 | async-start | bytes 262144 | tf_op jit(solution)/shard_map/all_to_all | solution.py:137
  116.8 70.7 %reduce-scatter.2.cloned.1.call-start = ((), (), s32[]{:S(2)}) async-start(), calls=%async_computation.5 | async-start | bytes 655360 | tf_op jit(solution)/shard_map/reduce_scatter | solution.py:154
Sparse Core Ops, SparseCore 0:
  166.8 20.6 reduce-scatter.1
where the time goes:
time: 197 us; the launch traced here: 196 us
  other arithmetic  44 us (22%)
  local copies, waits for them, and re-layouts  42.8 us (22%)
  waiting for transfers between devices  35.5 us (18%)
  starting transfers between devices  32.2 us (16%)
  matrix products  26.2 us (13%)
  between operations  15 us (8%)
    reduce_scatter x1, waiting for transfers between devices, shards(): update = lax.psum_scatter(gradient, 'ray', scatter_dimension=0, tiled=True)  19 us
    scatter-add x4, other arithmetic, forward_turn(): return partial_value.at[destined].add(product, mode='drop')  15 us
    scatter-add x4, other arithmetic, adjoint_turn(): return gradient.at[destined].add(product, mode='drop')  15 us
    dot_general x4, matrix products, forward_turn(): jnp.einsum('krp,kps->ksr', library[chosen], image_blocks[placed], preferr...  15 us
    dot_general x4, matrix products, adjoint_turn(): jnp.einsum('krp,ksr->kps', library[chosen], returned[sourced], preferred_...  10.4 us
    gather x4, local copies, waits for them, and re-layouts, forward_turn(): image_blocks[placed]  8.67 us
    gather x4, local copies, waits for them, and re-layouts, adjoint_turn(): library[chosen]  8.66 us
    gather x4, local copies, waits for them, and re-layouts, forward_turn(): library[chosen]  8.43 us
  transfers between devices with their start and end apart: 9, of which 5 were waited for; matrix products, arithmetic and copies ran while one was open for 31% of the time, Pallas kernels for 0%

commit v1 on v0

--- a/solution.py
+++ b/solution.py
@@ -1,6 +1,10 @@
+import functools
+
 import jax
 import jax.numpy as jnp
 from jax import lax
+from jax.experimental import pallas as pl
+from jax.experimental.pallas import tpu as pltpu
 from jax.sharding import PartitionSpec as P
 
 SMOOTH = 8
@@ -157,9 +161,428 @@
     return (residual, image_next)
 
 
+MESH = pl.DeviceIdType.MESH
+NT = (((1,), (1,)), ((), ()))
+NN = (((1,), (0,)), ((), ()))
+
+
+def dot(a, b, dims):
+    return lax.dot_general(a, b, dims, preferred_element_type=jnp.float32)
+
+
+def sort_pairs(count):
+    p = 1
+    while p < count:
+        k = p
+        while k >= 1:
+            for j in range(k % p, count - k, 2 * k):
+                for i in range(min(k, count - j - k)):
+                    if (i + j) // (2 * p) == (i + j + k) // (2 * p):
+                        yield i + j, i + j + k
+            k //= 2
+        p *= 2
+
+
+def step_kernel(
+    owners,
+    quarters,
+    taps_ref,
+    proj_ref,
+    image_ref,
+    library_ref,
+    entry_ref,
+    place_ref,
+    slot_ref,
+    count_ref,
+    carried_ref,
+    residual_ref,
+    update_ref,
+    rim,
+    phase_out,
+    phase_in,
+    shifted,
+    mixed,
+    partial_rows,
+    partial_out,
+    partial_in,
+    stripes,
+    forward,
+    blocks,
+    back_out,
+    back_in,
+    back_rows,
+    update_rows,
+    update_out,
+    update_in,
+    halo_send,
+    halo_recv,
+    phase_send,
+    phase_recv,
+    stripe_send,
+    stripe_recv,
+    partial_send,
+    partial_recv,
+    back_send,
+    back_recv,
+    update_send,
+    update_recv,
+):
+    f32, bf16 = jnp.float32, jnp.bfloat16
+    me, ray = lax.axis_index("dom"), lax.axis_index("ray")
+    slices, columns = proj_ref.shape
+    tile = library_ref.shape[-1]
+    entries = library_ref.shape[0]
+    places = image_ref.shape[1]
+    count = columns // tile
+    per = slices // owners
+    half = tile // 2
+    own_places = places // quarters
+
+    def dom_peer(k):
+        return lax.rem(me + k, owners)
+
+    def ray_peer(k):
+        return lax.rem(ray + k, quarters)
+
+    barrier = pltpu.get_barrier_semaphore()
+    for k in range(1, owners):
+        pl.semaphore_signal(barrier, inc=1, device_id=(dom_peer(k), ray), device_id_type=MESH)
+    for k in range(1, quarters):
+        pl.semaphore_signal(barrier, inc=1, device_id=(me, ray_peer(k)), device_id_type=MESH)
+
+    def dom_copy(src, dst, send, recv, k):
+        return pltpu.make_async_remote_copy(
+            src_ref=src,
+            dst_ref=dst,
+            send_sem=send.at[k],
+            recv_sem=recv.at[k],
+            device_id=(dom_peer(k), ray),
+            device_id_type=MESH,
+        )
+
+    def ray_copy(src, dst, send, recv, slot, k):
+        return pltpu.make_async_remote_copy(
+            src_ref=src,
+            dst_ref=dst,
+            send_sem=send.at[slot],
+            recv_sem=recv.at[slot],
+            device_id=(me, ray_peer(k)),
+            device_id_type=MESH,
+        )
+
+    for b in range(count):
+        rim[b + 1] = proj_ref[:, b * tile : (b + 1) * tile]
+    spread = jnp.broadcast_to(taps_ref[...], (tile, 2 * tile))
+    weights = pltpu.roll(spread, 0, 1, stride=1, stride_axis=0).astype(bf16)
+
+    pl.semaphore_wait(barrier, owners + quarters - 2)
+
+    halos = [
+        ray_copy(
+            proj_ref.at[:, pl.ds(columns - tile, tile)], rim.at[0], halo_send, halo_recv, 0, 1
+        ),
+        ray_copy(
+            proj_ref.at[:, pl.ds(0, tile)],
+            rim.at[count + 1],
+            halo_send,
+            halo_recv,
+            1,
+            quarters - 1,
+        ),
+    ]
+    for copy in halos:
+        copy.start()
+
+    capacity = entry_ref.shape[1]
+    slot = slot_ref[...]
+    relative = jnp.where(slot >= me, slot - me, slot - me + owners)
+    alive = lax.broadcasted_iota(jnp.int32, (1, capacity), 1) < count_ref[0, 0]
+    code = jnp.where(alive, entry_ref[...] * owners + relative, -1)
+    pick = jnp.where(
+        lax.broadcasted_iota(jnp.int32, (entries * owners, capacity), 0) == code, 1.0, 0.0
+    ).astype(bf16)
+    where_to = jnp.where(
+        lax.broadcasted_iota(jnp.int32, (places, capacity), 0) == place_ref[...], 1.0, 0.0
+    ).astype(bf16)
+    uses = dot(pick, where_to, NT).astype(bf16)
+    uses_back = dot(where_to, pick, NT).astype(bf16)
+
+    for copy in halos:
+        copy.wait()
+
+    @pl.when(ray == 0)
+    def _():
+        rim[0] = jnp.zeros((slices, tile), bf16)
+
+    @pl.when(ray == quarters - 1)
+    def _():
+        rim[count + 1] = jnp.zeros((slices, tile), bf16)
+
+    rows = (count + 1) * slices
+    phase = dot(rim[0 : count + 1].reshape(rows, tile), weights[:, :tile], NT)
+    phase = phase + dot(rim[1 : count + 2].reshape(rows, tile), weights[:, tile:], NT)
+    phase = phase.astype(bf16).astype(f32)
+    grouped = phase.reshape(count + 1, owners, per, tile)
+    for owner in range(owners):
+        phase_out[owner] = grouped[:, owner].astype(bf16)
+    phase_in[0] = phase_out[me]
+    phases = [
+        dom_copy(phase_out.at[dom_peer(k)], phase_in.at[k], phase_send, phase_recv, k)
+        for k in range(1, owners)
+    ]
+    for copy in phases:
+        copy.start()
+
+    turned = pltpu.roll(phase, half, 1).reshape(count + 1, slices, tile)
+    lane = lax.broadcasted_iota(jnp.int32, (1, 1, tile), 2)
+    shifted[...] = jnp.where(lane < half, turned[:count], turned[1:])
+
+    group = 8
+
+    def mix(step, carry):
+        for inner in range(group):
+            s = step * group + inner
+            mixed[s] = dot(uses, image_ref[s], NN).reshape(entries, owners, tile)
+        return carry
+
+    lax.fori_loop(0, slices // group, mix, 0)
+
+    total = jnp.zeros((slices * owners, tile), f32)
+    for entry in range(0, entries, 2):
+        left = jnp.concatenate(
+            [
+                mixed[:, entry].reshape(slices * owners, tile).astype(bf16),
+                mixed[:, entry + 1].reshape(slices * owners, tile).astype(bf16),
+            ],
+            axis=1,
+        )
+        right = jnp.concatenate([library_ref[entry], library_ref[entry + 1]], axis=1)
+        total = total + dot(left, right, NT)
+    partial_rows[...] = total
+    for k in range(1, owners):
+        partial_out[k] = partial_rows[pl.ds(k, slices, stride=owners), :].astype(bf16)
+    partial_in[me] = partial_rows[pl.ds(0, slices, stride=owners), :].astype(bf16)
+    partials = [
+        dom_copy(partial_out.at[k], partial_in.at[me], partial_send, partial_recv, k)
+        for k in range(1, owners)
+    ]
+
+    for copy in phases:
+        copy.wait_recv()
+
+    values = [phase_in[a].astype(f32) for a in range(owners)]
+    for i, j in sort_pairs(owners):
+        values[i], values[j] = jnp.minimum(values[i], values[j]), jnp.maximum(values[i], values[j])
+    middle = (values[owners // 2 - 1] + values[owners // 2]) * 0.5
+    profile = jnp.concatenate([middle[b] for b in range(count + 1)], axis=1)
+    width = columns + tile
+    detector = quarters * columns
+    position = ray * columns - half + lax.broadcasted_iota(jnp.int32, (1, width), 1)
+    profile = jnp.where((position >= 0) & (position < detector), profile, 0.0)
+    run = profile
+    reach = 1
+    while reach < 2 * SMOOTH:
+        run = run + pltpu.roll(run, reach, 1)
+        reach *= 2
+    window = pltpu.roll(run, width - (SMOOTH - 1), 1) + pltpu.roll(profile, width - SMOOTH, 1)
+    in_range = (
+        jnp.minimum(position + SMOOTH, detector - 1) - jnp.maximum(position - SMOOTH, 0) + 1
+    ).astype(f32)
+    stripe = pltpu.roll(profile - window / in_range, width - half, 1)
+    for b in range(count):
+        stripes[me, b] = stripe[:, b * tile : (b + 1) * tile].astype(bf16)
+    spreads = [
+        dom_copy(stripes.at[me], stripes.at[me], stripe_send, stripe_recv, k)
+        for k in range(1, owners)
+    ]
+    for copy in spreads:
+        copy.start()
+    for copy in partials:
+        copy.start()
+
+    for copy in partials:
+        copy.wait_recv()
+
+    def project(b, carry):
+        total = jnp.zeros((slices, tile), f32)
+        for d in range(owners):
+            share = jnp.where(carried_ref[0, d] == b, 1.0, 0.0).astype(f32)
+            total = total + share * partial_in[d].astype(f32)
+        forward[b] = total
+        return carry
+
+    lax.fori_loop(0, count, project, 0)
+
+    for copy in spreads:
+        copy.wait_recv()
+
+    for b in range(count):
+        stripe_all = jnp.concatenate([stripes[o, b].astype(f32) for o in range(owners)], axis=0)
+        corrected = (shifted[b] - stripe_all).astype(bf16).astype(f32)
+        rest = (corrected - forward[b]).astype(bf16)
+        blocks[b] = rest
+        residual_ref[:, b * tile : (b + 1) * tile] = rest
+
+    for k in range(1, owners):
+        back_out[k] = blocks[carried_ref[0, dom_peer(k)]]
+    backs = [
+        dom_copy(back_out.at[k], back_in.at[owners - k], back_send, back_recv, k)
+        for k in range(1, owners)
+    ]
+    for copy in backs:
+        copy.start()
+    back_in[0] = blocks[carried_ref[0, me]]
+    for copy in backs:
+        copy.wait_recv()
+
+    for k in range(owners):
+        back_rows[pl.ds(k, slices, stride=owners), :] = back_in[k].astype(f32)
+    gathered = back_rows[...].astype(bf16)
+    for entry in range(entries):
+        mixed[:, entry] = dot(gathered, library_ref[entry], NN).reshape(slices, owners, tile)
+
+    def unmix(step, carry):
+        for inner in range(group):
+            s = step * group + inner
+            piece = mixed[s].reshape(entries * owners, tile).astype(bf16)
+            start = pl.multiple_of(s * places, places)
+            update_rows[pl.ds(start, places), :] = dot(uses_back, piece, NN)
+        return carry
+
+    lax.fori_loop(0, slices // group, unmix, 0)
+    for place in range(places):
+        update_out[place // own_places, place % own_places] = update_rows[
+            pl.ds(place, slices, stride=places), :
+        ].astype(bf16)
+    updates = [
+        ray_copy(
+            update_out.at[ray_peer(k)], update_in.at[k], update_send, update_recv, k, k
+        )
+        for k in range(1, quarters)
+    ]
+    for copy in updates:
+        copy.start()
+    for copy in updates:
+        copy.wait_recv()
+    for place in range(own_places):
+        amount = update_out[ray, place].astype(f32)
+        for k in range(1, quarters):
+            amount = amount + update_in[k, place].astype(f32)
+        update_ref[place * tile : (place + 1) * tile, :] = amount.T
+    for copy in phases + partials + spreads + backs + updates:
+        copy.wait_send()
+
+
+def fast_shards(
+    projections,
+    phase_kernel,
+    image,
+    tile_library,
+    tile_entry,
+    tile_image,
+    tile_slot,
+    tile_count,
+    slot_block,
+):
+    f32, bf16 = jnp.float32, jnp.bfloat16
+    owners, quarters = lax.axis_size("dom"), lax.axis_size("ray")
+    entries, tile = tile_library.shape[2], tile_library.shape[-1]
+    _, slices, columns = projections.shape
+    count = columns // tile
+    places = image.shape[0] // tile
+    per = slices // owners
+    own_places = places // quarters
+    taps = jnp.pad(phase_kernel.astype(f32), (0, 2 * tile - phase_kernel.shape[0]))[None]
+    by_slice = image.reshape(places, tile, slices).transpose(2, 0, 1)
+    vmem = pl.BlockSpec(memory_space=pltpu.VMEM)
+    smem = pl.BlockSpec(memory_space=pltpu.SMEM)
+    sems = pltpu.SemaphoreType.DMA
+    residual, update = pl.pallas_call(
+        functools.partial(step_kernel, owners, quarters),
+        out_shape=(
+            jax.ShapeDtypeStruct((slices, columns), bf16),
+            jax.ShapeDtypeStruct((own_places * tile, slices), f32),
+        ),
+        in_specs=[vmem] * 7 + [smem] * 2,
+        out_specs=(vmem, vmem),
+        scratch_shapes=[
+            pltpu.VMEM((count + 2, slices, tile), bf16),
+            pltpu.VMEM((owners, count + 1, per, tile), bf16),
+            pltpu.VMEM((owners, count + 1, per, tile), bf16),
+            pltpu.VMEM((count, slices, tile), f32),
+            pltpu.VMEM((slices, entries, owners, tile), f32),
+            pltpu.VMEM((slices * owners, tile), f32),
+            pltpu.VMEM((owners, slices, tile), bf16),
+            pltpu.VMEM((owners, slices, tile), bf16),
+            pltpu.VMEM((owners, count, per, tile), bf16),
+            pltpu.VMEM((count, slices, tile), f32),
+            pltpu.VMEM((count, slices, tile), bf16),
+            pltpu.VMEM((owners, slices, tile), bf16),
+            pltpu.VMEM((owners, slices, tile), bf16),
+            pltpu.VMEM((slices * owners, tile), f32),
+            pltpu.VMEM((slices * places, tile), f32),
+            pltpu.VMEM((quarters, own_places, slices, tile), bf16),
+            pltpu.VMEM((quarters, own_places, slices, tile), bf16),
+            sems((2,)),
+            sems((2,)),
+            sems((owners,)),
+            sems((owners,)),
+            sems((owners,)),
+            sems((owners,)),
+            sems((owners,)),
+            sems((owners,)),
+            sems((owners,)),
+            sems((owners,)),
+            sems((quarters,)),
+            sems((quarters,)),
+        ],
+        compiler_params=pltpu.CompilerParams(
+            collective_id=0, has_side_effects=True, vmem_limit_bytes=48 * 1024 * 1024
+        ),
+    )(
+        taps,
+        projections[0],
+        by_slice,
+        tile_library[0, 0],
+        tile_entry[0],
+        tile_image[0],
+        tile_slot[0],
+        tile_count,
+        slot_block[0],
+    )
+    rows_own = own_places * tile
+    own_image = lax.dynamic_slice_in_dim(image, lax.axis_index("ray") * rows_own, rows_own)
+    return residual[None], own_image.astype(f32) + relax_factor * update
+
+
+def fits_kernel(projections, phase_kernel, image, tile_library, tile_entry, *rest):
+    owners, quarters = lax.axis_size("dom"), lax.axis_size("ray")
+    tile = tile_library.shape[-1]
+    angles, slices, columns = projections.shape
+    return (
+        angles == 1
+        and slices % 16 == 0
+        and slices == 8 * owners
+        and owners == 8
+        and tile == 128
+        and phase_kernel.shape[0] == tile + 1
+        and columns % tile == 0
+        and tile_library.shape[2] % 2 == 0
+        and (image.shape[0] // tile) % (16 * 1) == 0
+        and (image.shape[0] // tile) % quarters == 0
+        and tile_entry.shape[2] <= 256
+    )
+
+
+def any_shards(*args):
+    if fits_kernel(*args):
+        return fast_shards(*args)
+    return shards(*args)
+
+
 def solution(mesh):
     return jax.shard_map(
-        shards,
+        any_shards,
         mesh=mesh,
         in_specs=(
             P("dom", None, "ray"),

time: 197 us -> 47.6 us (0.24)
  other arithmetic: 44 us -> 0.75 us
  Pallas kernels: 0 us -> 40.2 us
  local copies, waits for them, and re-layouts: 42.8 us -> 5.03 us
  waiting for transfers between devices: 35.5 us -> 0 us
  starting transfers between devices: 32.2 us -> 0 us
  matrix products: 26.2 us -> 0 us
  between operations: 15 us -> 1.39 us
    pallas_call x0 -> x1, Pallas kernels: none -> 40.2 us  [fast_shards(): pl.pallas_call(functools.partial(step_kernel, owners, quarters), out_shap...]
    gather x16 -> x0, local copies, waits for them, and re-layouts: 32.4 us -> none  [the longest x4 8.67 us: forward_turn(): image_blocks[placed]]
    scatter-add x8 -> x0, other arithmetic: 30.1 us -> none  [the longest x4 15 us: forward_turn(): return partial_value.at[destined].add(product, mode='drop')]
    dot_general x11 -> x0, matrix products: 26.2 us -> none  [the longest x4 15 us: forward_turn(): jnp.einsum('krp,kps->ksr', library[chosen], image_blocks[placed], preferr...]
    all_to_all x4 -> x0, starting transfers between devices: 23.1 us -> none  [the longest x1 6.43 us: shards(): lax.all_to_all(phase, 'dom', split_axis=1, concat_axis=0, tiled=True)]
    reduce_scatter x1 -> x0, waiting for transfers between devices: 19 us -> none  [shards(): update = lax.psum_scatter(gradient, 'ray', scatter_dimension=0, tiled=True)]
    all_to_all x4 -> x0, waiting for transfers between devices: 15.5 us -> none  [the longest x1 8.09 us: shards(): lax.all_to_all(fixed_rows, 'dom', split_axis=0, concat_axis=1, tiled=True)]
    ppermute x4 -> x0, starting transfers between devices: 9.02 us -> none  [the longest x2 6.44 us: with_halo(): lax.ppermute(tail, axis, [(i, (i + 1) % count) for i in range(ends)])]
  transfers between devices with their start and end apart: 9 -> 0, of which waited for: 5 -> 0; matrix products, arithmetic and copies ran while one was open for 31% -> 0% of each run, Pallas kernels for 0% -> 0%
where the time goes in v1:
time: 47.6 us; the launch traced here: 47.3 us
  Pallas kernels  40.2 us (84%)
  local copies, waits for them, and re-layouts  5.03 us (11%)
  between operations  1.39 us (3%)
  other arithmetic  0.75 us (2%)
    pallas_call x1, Pallas kernels, fast_shards(): pl.pallas_call(functools.partial(step_kernel, owners, quarters), out_shap...  40.2 us
    unnamed x16, local copies, waits for them, and re-layouts  4.18 us

profile of v1, /device:TPU:0, one launch (start us, length us, event | category | flops | bytes accessed | tf_op | source)
XLA Modules:
  0.0 47.3 jit_solution(17038691236093264625)
XLA Ops:
  0.6 0.0 copy-start
  0.6 0.7 %pad_convert_fusion = f32[256]{0:T(256)S(1)} fusion(bf16[129]{0:T(256)(128)(2,1)} %param.10), kind=kLoop, calls=%fused_computation.1 | loop fusion | flops 256 | bytes 1282 | tf_op jit(solution)/shard_map/broadcast_in_dim | solution.py:495
  1.4 1.0 %copy.14 = bf16[8,8,16,128]{3,2,1,0:T(8,128)(2,1)S(1)} copy(bf16[8,8,16,128]{3,1,2,0:T(8,128)(2,1)} %bitcast.23) | data formatting | bytes 524288
  2.3 0.0 copy-start.3
  2.4 0.0 copy-start.4
  3.0 0.0 copy-start.2
  3.0 0.0 copy-start.5
  3.1 0.0 copy-done
  3.1 0.0 copy-done.3
  3.1 0.0 copy-done.4
  3.1 0.6 %copy-done.2 = s32[1,1,256]{2,1,0:T(1,128)S(1)} copy-done((s32[1,1,256]{2,1,0:T(1,128)S(1)}, s32[1,1,256]{2,1,0:T(1,128)}, u32[]{:S(2)}) %copy-start.2) | copy-done | bytes 1048
  3.7 0.0 copy-done.5
  3.7 0.0 copy-start.1
  3.7 0.9 %copy-done.1 = bf16[1,64,2048]{2,1,0:T(8,128)(2,1)S(1)} copy-done((bf16[1,64,2048]{2,1,0:T(8,128)(2,1)S(1)}, bf16[1,64,2048]{2,1,0:T(8,128)(2,1)}, u32[]{:S(2)}) %copy-start.1) | copy-done | bytes 262168
  4.7 40.2 %shard_map.104 = (bf16[64,2048]{1,0:T(8,128)(2,1)S(1)}, f32[512,64]{1,0:T(8,128)S(1)}) custom-call(f32[1,256]{1,0:T(1,128)S(1)} %bitcast.21, bf16[64,2048]{1,0:T(8,128)(2,1)S(1)} %bitcast.16, bf16[64,16,128]{2,1,0:T(8,128)(2,1)S(1)} %bitcast.14, bf16[16,128,128]{2,1,0:T(8,128)(2,1)S(1)} %bitcast.15, s32[1,256]{1,0:T(1,128)S(1)} %bitcast.18, ...), custom_call_target="tpu_custom_call" | custom-call | tf_op jit(solution)/shard_map/pallas_call | solution.py:500
  44.8 0.8 %constant_dynamic-slice_fusion = bf16[512,64]{0,1:T(8,128)(2,1)S(1)} fusion(bf16[2048,64]{0,1:T(8,128)(2,1)} %param.11, s32[]{:T(128)S(6)} %select_n.3), kind=kLoop, calls=%fused_computation.2 | loop fusion | bytes 131076 | tf_op jit(solution)/shard_map/dynamic_slice | solution.py:554
  45.7 0.1 copy.13
  45.8 0.8 %copy.12 = f32[512,64]{0,1:T(8,128)} copy(f32[512,64]{1,0:T(8,128)S(1)} %multiply_add_fusion) | data formatting | bytes 262144
  46.6 0.7 %copy.17 = bf16[1,64,2048]{2,1,0:T(8,128)(2,1)} copy(bf16[1,64,2048]{2,1,0:T(8,128)(2,1)S(1)} %bitcast.17) | data formatting | bytes 524288
  (1 shorter events, 0.0 us)
Async XLA Ops:
  0.6 2.4 %copy-start = (bf16[1,1,16,128,128]{4,3,2,1,0:T(8,128)(2,1)S(1)}, bf16[1,1,16,128,128]{4,3,2,1,0:T(8,128)(2,1)}, u32[]{:S(2)}) copy-start(bf16[1,1,16,128,128]{4,3,2,1,0:T(8,128)(2,1)} %param.12) | copy-start | bytes 1572868
  2.3 0.7 %copy-start.3 = (s32[1,1,256]{2,1,0:T(1,128)S(1)}, s32[1,1,256]{2,1,0:T(1,128)}, u32[]{:S(2)}) copy-start(s32[1,1,256]{2,1,0:T(1,128)} %param.14) | copy-start | bytes 3076
  2.4 0.7 %copy-start.4 = (s32[1,1,256]{2,1,0:T(1,128)S(1)}, s32[1,1,256]{2,1,0:T(1,128)}, u32[]{:S(2)}) copy-start(s32[1,1,256]{2,1,0:T(1,128)} %param.15) | copy-start | bytes 3076
  3.0 0.7 %copy-start.2 = (s32[1,1,256]{2,1,0:T(1,128)S(1)}, s32[1,1,256]{2,1,0:T(1,128)}, u32[]{:S(2)}) copy-start(s32[1,1,256]{2,1,0:T(1,128)} %param.13) | copy-start | bytes 3076
  3.0 0.7 %copy-start.5 = (s32[1,1,8]{2,1,0:T(1,128)S(1)}, s32[1,1,8]{2,1,0:T(1,128)}, u32[]{:S(2)}) copy-start(s32[1,1,8]{2,1,0:T(1,128)} %param.17) | copy-start | bytes 100
  3.7 1.0 %copy-start.1 = (bf16[1,64,2048]{2,1,0:T(8,128)(2,1)S(1)}, bf16[1,64,2048]{2,1,0:T(8,128)(2,1)}, u32[]{:S(2)}) copy-start(bf16[1,64,2048]{2,1,0:T(8,128)(2,1)} %param.9) | copy-start | bytes 786436

commit v2 on v1

--- a/solution.py
+++ b/solution.py
@@ -187,16 +187,16 @@
     owners,
     quarters,
     taps_ref,
-    proj_ref,
-    image_ref,
-    library_ref,
+    proj_any,
+    image_any,
+    library_any,
     entry_ref,
     place_ref,
     slot_ref,
     count_ref,
     carried_ref,
     residual_ref,
-    update_ref,
+    next_ref,
     rim,
     phase_out,
     phase_in,
@@ -226,13 +226,19 @@
     back_recv,
     update_send,
     update_recv,
+    taps_wide,
+    proj_ref,
+    image_rows,
+    image_ref,
+    library_ref,
+    load_sem,
 ):
     f32, bf16 = jnp.float32, jnp.bfloat16
     me, ray = lax.axis_index("dom"), lax.axis_index("ray")
     slices, columns = proj_ref.shape
     tile = library_ref.shape[-1]
     entries = library_ref.shape[0]
-    places = image_ref.shape[1]
+    places = image_rows.shape[0] // tile
     count = columns // tile
     per = slices // owners
     half = tile // 2
@@ -243,6 +249,14 @@
 
     def ray_peer(k):
         return lax.rem(ray + k, quarters)
+
+    loads = [
+        pltpu.make_async_copy(proj_any.at[0], proj_ref, load_sem.at[0]),
+        pltpu.make_async_copy(image_any, image_rows, load_sem.at[1]),
+        pltpu.make_async_copy(library_any.at[0, 0], library_ref, load_sem.at[2]),
+    ]
+    for copy in loads:
+        copy.start()
 
     barrier = pltpu.get_barrier_semaphore()
     for k in range(1, owners):
@@ -270,11 +284,12 @@
             device_id_type=MESH,
         )
 
-    for b in range(count):
-        rim[b + 1] = proj_ref[:, b * tile : (b + 1) * tile]
-    spread = jnp.broadcast_to(taps_ref[...], (tile, 2 * tile))
+    taps_wide[...] = jnp.zeros((1, 2 * tile), f32)
+    taps_wide[:, : taps_ref.shape[1]] = taps_ref[...].astype(f32)
+    spread = jnp.broadcast_to(taps_wide[...], (tile, 2 * tile))
     weights = pltpu.roll(spread, 0, 1, stride=1, stride_axis=0).astype(bf16)
 
+    loads[0].wait()
     pl.semaphore_wait(barrier, owners + quarters - 2)
 
     halos = [
@@ -307,6 +322,49 @@
     uses = dot(pick, where_to, NT).astype(bf16)
     uses_back = dot(where_to, pick, NT).astype(bf16)
 
+    for b in range(count):
+        rim[b + 1] = proj_ref[:, b * tile : (b + 1) * tile]
+    loads[1].wait()
+    for place in range(places):
+        image_ref[pl.ds(place, slices, stride=places), :] = (
+            image_rows[place * tile : (place + 1) * tile, :].astype(f32).T
+        )
+
+    group = 8
+
+    def mix(step, carry):
+        for inner in range(group):
+            s = step * group + inner
+            start = pl.multiple_of(s * places, places)
+            piece = image_ref[pl.ds(start, places), :].astype(bf16)
+            mixed[s] = dot(uses, piece, NN).reshape(entries, owners, tile)
+        return carry
+
+    lax.fori_loop(0, slices // group, mix, 0)
+
+    loads[2].wait()
+    total = jnp.zeros((slices * owners, tile), f32)
+    for entry in range(0, entries, 2):
+        left = jnp.concatenate(
+            [
+                mixed[:, entry].reshape(slices * owners, tile).astype(bf16),
+                mixed[:, entry + 1].reshape(slices * owners, tile).astype(bf16),
+            ],
+            axis=1,
+        )
+        right = jnp.concatenate([library_ref[entry], library_ref[entry + 1]], axis=1)
+        total = total + dot(left, right, NT)
+    partial_rows[...] = total
+    for k in range(1, owners):
+        partial_out[k] = partial_rows[pl.ds(k, slices, stride=owners), :].astype(bf16)
+    partial_in[me] = partial_rows[pl.ds(0, slices, stride=owners), :].astype(bf16)
+    partials = [
+        dom_copy(partial_out.at[k], partial_in.at[me], partial_send, partial_recv, k)
+        for k in range(1, owners)
+    ]
+    for copy in partials:
+        copy.start()
+
     for copy in halos:
         copy.wait()
 
@@ -336,36 +394,6 @@
     turned = pltpu.roll(phase, half, 1).reshape(count + 1, slices, tile)
     lane = lax.broadcasted_iota(jnp.int32, (1, 1, tile), 2)
     shifted[...] = jnp.where(lane < half, turned[:count], turned[1:])
-
-    group = 8
-
-    def mix(step, carry):
-        for inner in range(group):
-            s = step * group + inner
-            mixed[s] = dot(uses, image_ref[s], NN).reshape(entries, owners, tile)
-        return carry
-
-    lax.fori_loop(0, slices // group, mix, 0)
-
-    total = jnp.zeros((slices * owners, tile), f32)
-    for entry in range(0, entries, 2):
-        left = jnp.concatenate(
-            [
-                mixed[:, entry].reshape(slices * owners, tile).astype(bf16),
-                mixed[:, entry + 1].reshape(slices * owners, tile).astype(bf16),
-            ],
-            axis=1,
-        )
-        right = jnp.concatenate([library_ref[entry], library_ref[entry + 1]], axis=1)
-        total = total + dot(left, right, NT)
-    partial_rows[...] = total
-    for k in range(1, owners):
-        partial_out[k] = partial_rows[pl.ds(k, slices, stride=owners), :].astype(bf16)
-    partial_in[me] = partial_rows[pl.ds(0, slices, stride=owners), :].astype(bf16)
-    partials = [
-        dom_copy(partial_out.at[k], partial_in.at[me], partial_send, partial_recv, k)
-        for k in range(1, owners)
-    ]
 
     for copy in phases:
         copy.wait_recv()
@@ -391,13 +419,22 @@
     stripe = pltpu.roll(profile - window / in_range, width - half, 1)
     for b in range(count):
         stripes[me, b] = stripe[:, b * tile : (b + 1) * tile].astype(bf16)
-    spreads = [
-        dom_copy(stripes.at[me], stripes.at[me], stripe_send, stripe_recv, k)
-        for k in range(1, owners)
-    ]
+    steps = owners // 2
+    beside = 1 - 2 * lax.rem(me, 2)
+
+    def stripe_copy(source, k, slot):
+        return pltpu.make_async_remote_copy(
+            src_ref=stripes.at[source],
+            dst_ref=stripes.at[source],
+            send_sem=stripe_send.at[slot],
+            recv_sem=stripe_recv.at[slot],
+            device_id=(lax.rem(me + k + owners, owners), ray),
+            device_id_type=MESH,
+        )
+
+    spreads = [stripe_copy(me, 2 * k, k) for k in range(1, steps)]
+    spreads = spreads + [stripe_copy(me, beside, 0)]
     for copy in spreads:
-        copy.start()
-    for copy in partials:
         copy.start()
 
     for copy in partials:
@@ -413,7 +450,13 @@
 
     lax.fori_loop(0, count, project, 0)
 
-    for copy in spreads:
+    spreads[-1].wait_recv()
+    relays = []
+    for k in range(1, steps):
+        spreads[k - 1].wait_recv()
+        relays.append(stripe_copy(lax.rem(me - 2 * k + owners, owners), beside, steps + k))
+        relays[-1].start()
+    for copy in relays:
         copy.wait_recv()
 
     for b in range(count):
@@ -437,39 +480,59 @@
 
     for k in range(owners):
         back_rows[pl.ds(k, slices, stride=owners), :] = back_in[k].astype(f32)
-    gathered = back_rows[...].astype(bf16)
-    for entry in range(entries):
-        mixed[:, entry] = dot(gathered, library_ref[entry], NN).reshape(slices, owners, tile)
-
-    def unmix(step, carry):
-        for inner in range(group):
-            s = step * group + inner
-            piece = mixed[s].reshape(entries * owners, tile).astype(bf16)
-            start = pl.multiple_of(s * places, places)
-            update_rows[pl.ds(start, places), :] = dot(uses_back, piece, NN)
-        return carry
-
-    lax.fori_loop(0, slices // group, unmix, 0)
-    for place in range(places):
-        update_out[place // own_places, place % own_places] = update_rows[
-            pl.ds(place, slices, stride=places), :
-        ].astype(bf16)
-    updates = [
-        ray_copy(
-            update_out.at[ray_peer(k)], update_in.at[k], update_send, update_recv, k, k
-        )
-        for k in range(1, quarters)
-    ]
-    for copy in updates:
-        copy.start()
+    parts = update_out.shape[0]
+    part = slices // parts
+    updates = []
+    for turn in range(parts):
+        rows = part * owners
+        gathered = back_rows[turn * rows : (turn + 1) * rows, :].astype(bf16)
+        first = turn * part
+        for entry in range(entries):
+            mixed[first : first + part, entry] = dot(gathered, library_ref[entry], NN).reshape(
+                part, owners, tile
+            )
+
+        def unmix(step, carry, first=first):
+            for inner in range(group):
+                s = first + step * group + inner
+                piece = mixed[s].reshape(entries * owners, tile).astype(bf16)
+                start = pl.multiple_of(s * places, places)
+                update_rows[pl.ds(start, places), :] = dot(uses_back, piece, NN)
+            return carry
+
+        lax.fori_loop(0, part // group, unmix, 0)
+        for place in range(places):
+            update_out[turn, place // own_places, place % own_places] = update_rows[
+                pl.ds(first * places + place, part, stride=places), :
+            ].astype(bf16)
+        sent = [
+            ray_copy(
+                update_out.at[turn, ray_peer(k)],
+                update_in.at[turn, k],
+                update_send,
+                update_recv,
+                turn * quarters + k,
+                k,
+            )
+            for k in range(1, quarters)
+        ]
+        for copy in sent:
+            copy.start()
+        updates = updates + sent
     for copy in updates:
         copy.wait_recv()
     for place in range(own_places):
-        amount = update_out[ray, place].astype(f32)
-        for k in range(1, quarters):
-            amount = amount + update_in[k, place].astype(f32)
-        update_ref[place * tile : (place + 1) * tile, :] = amount.T
-    for copy in phases + partials + spreads + backs + updates:
+        amounts = []
+        for turn in range(parts):
+            amount = update_out[turn, ray, place].astype(f32)
+            for k in range(1, quarters):
+                amount = amount + update_in[turn, k, place].astype(f32)
+            amounts.append(amount)
+        update = jnp.concatenate(amounts, axis=0).T
+        start = pl.multiple_of((ray * own_places + place) * tile, tile)
+        held = image_rows[pl.ds(start, tile), :].astype(f32)
+        next_ref[place * tile : (place + 1) * tile, :] = held + relax_factor * update
+    for copy in phases + partials + spreads + relays + backs + updates:
         copy.wait_send()
 
 
@@ -492,18 +555,18 @@
     places = image.shape[0] // tile
     per = slices // owners
     own_places = places // quarters
-    taps = jnp.pad(phase_kernel.astype(f32), (0, 2 * tile - phase_kernel.shape[0]))[None]
-    by_slice = image.reshape(places, tile, slices).transpose(2, 0, 1)
+    parts = 2
+    hbm = pl.BlockSpec(memory_space=pl.ANY)
     vmem = pl.BlockSpec(memory_space=pltpu.VMEM)
     smem = pl.BlockSpec(memory_space=pltpu.SMEM)
     sems = pltpu.SemaphoreType.DMA
-    residual, update = pl.pallas_call(
+    residual, image_next = pl.pallas_call(
         functools.partial(step_kernel, owners, quarters),
         out_shape=(
             jax.ShapeDtypeStruct((slices, columns), bf16),
             jax.ShapeDtypeStruct((own_places * tile, slices), f32),
         ),
-        in_specs=[vmem] * 7 + [smem] * 2,
+        in_specs=[vmem] + [hbm] * 3 + [vmem] * 3 + [smem] * 2,
         out_specs=(vmem, vmem),
         scratch_shapes=[
             pltpu.VMEM((count + 2, slices, tile), bf16),
@@ -521,8 +584,8 @@
             pltpu.VMEM((owners, slices, tile), bf16),
             pltpu.VMEM((slices * owners, tile), f32),
             pltpu.VMEM((slices * places, tile), f32),
-            pltpu.VMEM((quarters, own_places, slices, tile), bf16),
-            pltpu.VMEM((quarters, own_places, slices, tile), bf16),
+            pltpu.VMEM((parts, quarters, own_places, slices // parts, tile), bf16),
+            pltpu.VMEM((parts, quarters, own_places, slices // parts, tile), bf16),
             sems((2,)),
             sems((2,)),
             sems((owners,)),
@@ -533,26 +596,30 @@
             sems((owners,)),
             sems((owners,)),
             sems((owners,)),
-            sems((quarters,)),
-            sems((quarters,)),
+            sems((parts * quarters,)),
+            sems((parts * quarters,)),
+            pltpu.VMEM((1, 2 * tile), f32),
+            pltpu.VMEM((slices, columns), bf16),
+            pltpu.VMEM(image.shape, bf16),
+            pltpu.VMEM((slices * places, tile), f32),
+            pltpu.VMEM((entries, tile, tile), bf16),
+            sems((3,)),
         ],
         compiler_params=pltpu.CompilerParams(
             collective_id=0, has_side_effects=True, vmem_limit_bytes=48 * 1024 * 1024
         ),
     )(
-        taps,
-        projections[0],
-        by_slice,
-        tile_library[0, 0],
+        phase_kernel[None],
+        projections,
+        image,
+        tile_library,
         tile_entry[0],
         tile_image[0],
         tile_slot[0],
         tile_count,
         slot_block[0],
     )
-    rows_own = own_places * tile
-    own_image = lax.dynamic_slice_in_dim(image, lax.axis_index("ray") * rows_own, rows_own)
-    return residual[None], own_image.astype(f32) + relax_factor * update
+    return residual[None], image_next
 
 
 def fits_kernel(projections, phase_kernel, image, tile_library, tile_entry, *rest):

time: 47.6 us -> 44.2 us (0.929)
  local copies, waits for them, and re-layouts: 5.03 us -> 3.42 us
  Pallas kernels: 40.2 us -> 39.2 us
  other arithmetic: 0.75 us -> 0 us
    unnamed x16 -> x15, local copies, waits for them, and re-layouts: 4.18 us -> 2.76 us
    pallas_call x1, Pallas kernels: 40.2 us -> 39.2 us  [fast_shards(): pl.pallas_call(functools.partial(step_kernel, owners, quarters), out_shap...]
    dynamic_slice x1 -> x0, local copies, waits for them, and re-layouts: 0.85 us -> none  [fast_shards(): lax.dynamic_slice_in_dim(image, lax.axis_index('ray') * rows_own, rows_own)]
    broadcast_in_dim x1 -> x0, other arithmetic: 0.72 us -> none  [fast_shards(): jnp.pad(phase_kernel.astype(f32), (0, 2 * tile - phase_kernel.shape[0]))]
    broadcast_in_dim x0 -> x1, local copies, waits for them, and re-layouts: none -> 0.66 us  [fast_shards(): phase_kernel[None]]
where the time goes in v2:
time: 44.2 us; the launch traced here: 44 us
  Pallas kernels  39.2 us (89%)
  local copies, waits for them, and re-layouts  3.42 us (8%)
  between operations  1.42 us (3%)
    pallas_call x1, Pallas kernels, fast_shards(): pl.pallas_call(functools.partial(step_kernel, owners, quarters), out_shap...  39.2 us
    unnamed x15, local copies, waits for them, and re-layouts  2.76 us

profile of v2, /device:TPU:0, one launch (start us, length us, event | category | flops | bytes accessed | tf_op | source)
XLA Modules:
  0.0 44.0 jit_solution(9278697744062260642)
XLA Ops:
  0.6 0.0 copy-start
  1.3 0.7 %broadcast_in_dim.6.taps_ref = bf16[1,129]{1,0:T(2,128)(2,1)S(1)} reshape(bf16[129]{0:T(256)(128)(2,1)} %param.10) | data formatting | bytes 516 | tf_op jit(solution)/shard_map/broadcast_in_dim | solution.py:612
  2.0 0.0 copy-start.1
  2.0 0.0 copy-start.2
  2.0 0.0 copy-start.3
  2.0 0.0 copy-start.4
  2.0 0.0 copy-start.5
  2.0 1.3 %copy.11.image_any = bf16[2048,64]{1,0:T(8,128)(2,1)S(1)} copy(bf16[2048,64]{0,1:T(8,128)(2,1)} %param.11) | data formatting | bytes 524288 | tf_op args[2]
  3.3 0.0 copy-done
  3.3 0.0 copy-done.1
  3.3 0.0 copy-done.2
  3.3 0.0 copy-done.3
  3.3 0.0 copy-done.4
  3.3 0.0 copy-done.5
  3.4 39.2 %shard_map.104 = (bf16[64,2048]{1,0:T(8,128)(2,1)S(1)}, f32[512,64]{1,0:T(8,128)S(1)}) custom-call(bf16[1,129]{1,0:T(2,128)(2,1)S(1)} %broadcast_in_dim.6.taps_ref, bf16[1,64,2048]{2,1,0:T(8,128)(2,1)S(1)} %copy-done.1, bf16[2048,64]{1,0:T(8,128)(2,1)S(1)} %copy.11.image_any, bf16[1,1,16,128,128]{4,3,2,1,0:T(8,128)(2,1)S(1)} %copy-done, ...), custom_call_target="tpu_custom_call" | custom-call | tf_op jit(solution)/shard_map/pallas_call | solution.py:563
  42.5 0.8 %copy.12 = f32[512,64]{0,1:T(8,128)} copy(f32[512,64]{1,0:T(8,128)S(1)} %get-tuple-element.7) | data formatting | bytes 262144
  43.3 0.7 %copy.15 = bf16[1,64,2048]{2,1,0:T(8,128)(2,1)} copy(bf16[1,64,2048]{2,1,0:T(8,128)(2,1)S(1)} %bitcast.5) | data formatting | bytes 524288
Async XLA Ops:
  0.6 2.7 %copy-start = (bf16[1,1,16,128,128]{4,3,2,1,0:T(8,128)(2,1)S(1)}, bf16[1,1,16,128,128]{4,3,2,1,0:T(8,128)(2,1)}, u32[]{:S(2)}) copy-start(bf16[1,1,16,128,128]{4,3,2,1,0:T(8,128)(2,1)} %library_any.1) | copy-start | bytes 1572868
  2.0 1.3 %copy-start.1 = (bf16[1,64,2048]{2,1,0:T(8,128)(2,1)S(1)}, bf16[1,64,2048]{2,1,0:T(8,128)(2,1)}, u32[]{:S(2)}) copy-start(bf16[1,64,2048]{2,1,0:T(8,128)(2,1)} %proj_any.1) | copy-start | bytes 786436
  2.0 1.3 %copy-start.2 = (s32[1,1,256]{2,1,0:T(1,128)S(1)}, s32[1,1,256]{2,1,0:T(1,128)}, u32[]{:S(2)}) copy-start(s32[1,1,256]{2,1,0:T(1,128)} %param.13) | copy-start | bytes 3076
  2.0 1.3 %copy-start.3 = (s32[1,1,256]{2,1,0:T(1,128)S(1)}, s32[1,1,256]{2,1,0:T(1,128)}, u32[]{:S(2)}) copy-start(s32[1,1,256]{2,1,0:T(1,128)} %param.14) | copy-start | bytes 3076
  2.0 1.3 %copy-start.4 = (s32[1,1,256]{2,1,0:T(1,128)S(1)}, s32[1,1,256]{2,1,0:T(1,128)}, u32[]{:S(2)}) copy-start(s32[1,1,256]{2,1,0:T(1,128)} %param.15) | copy-start | bytes 3076
  2.0 1.3 %copy-start.5 = (s32[1,1,8]{2,1,0:T(1,128)S(1)}, s32[1,1,8]{2,1,0:T(1,128)}, u32[]{:S(2)}) copy-start(s32[1,1,8]{2,1,0:T(1,128)} %param.17) | copy-start | bytes 100
